TPU v7x, 512 devices: a 4x2x32 block of a 4x8x32 slice. The times are simulated.
512 devices in a mesh: groups: 2 (over y), dp: 4 (over x), tensor: 64 (over z, core).
Axes of the slice: x: 4, y: 2, z: 32, core: 2. Of those that a mesh axis runs over, the one named last changes fastest.
The devices are a block of a 4x8x32 slice.
Arguments:
- tokens: bfloat16 [1024, 8192], P(('groups', 'dp'), 'tensor'), parts along dimension 0, may hold values from -6 to 6
- gate_up_weight: bfloat16 [8192, 32768], P('dp', 'tensor'), may hold values from -0.0625 to 0.0625
- down_weight: bfloat16 [16384, 8192], P('tensor', 'dp'), may hold values from -0.046875 to 0.046875
Outputs:
- mixed_out: bfloat16 [1024, 8192], P(('groups', 'dp'), 'tensor'), parts along dimension 0
There are 2 independent parts, one for each index of `groups`. A program takes and returns all parts, laid end to end along the dimension named above; an argument that names none is the same for every part. Nothing has to cross between parts.
All inputs are finite; a program needn't handle non-finite values.
Results may differ from a plain program's by a relative error of at most 0.0049.
Values may be sent and summed in bfloat16 or wider, within the bound.
No kernel may reach another device: no remote copies, remote signals or barrier semaphores. Data moves between devices by JAX's collectives and lax.ppermute only.
A program may use at most 64 MiB of HBM per device.

v0:
```python
import jax
import jax.numpy as jnp
from jax import lax
from jax.sharding import Mesh
from jax.sharding import PartitionSpec as P

TENSOR = ("tensor_0", "tensor_1")


def split_up(array, dim, devices):
    lengths = array.shape
    pieces = array.reshape(*lengths[:dim], devices, lengths[dim] // devices, *lengths[dim + 1 :])
    return jnp.moveaxis(pieces, dim, 0)


def summed_on_arrival(array, axis, dim):
    pieces = split_up(array, dim, lax.axis_size(axis))
    arrived = lax.all_to_all(pieces, axis, split_axis=0, concat_axis=0, tiled=True)
    return arrived.sum(axis=0)


def reduced_to_own(pieces, axes, turns):
    lengths = [lax.axis_size(a) for a in axes]
    pieces = pieces.reshape(*lengths, *pieces.shape[1:])
    pieces = pieces.transpose(*turns, *range(len(axes), pieces.ndim))
    pieces = pieces.reshape(-1, *pieces.shape[len(axes) :])
    for k in turns:
        pieces = lax.psum_scatter(pieces, axes[k], scatter_dimension=0, tiled=True)
    return pieces[0]


def summed_rows(array, axes, turns, dim):
    devices = lax.axis_size(axes)
    return reduced_to_own(split_up(array, dim, devices), axes, turns)


def per_device(tokens, gate_up_weight, down_weight):
    whole = lax.all_gather(tokens, TENSOR, axis=1, tiled=True)
    blocks = lax.all_to_all(whole, "dp", split_axis=1, concat_axis=0, tiled=True)
    partial_value = jnp.dot(blocks, gate_up_weight, preferred_element_type=jnp.float32)
    combined = summed_on_arrival(partial_value, "dp", 0)
    gate_part = combined[:, 0::2]
    up_part = combined[:, 1::2]
    hidden = (jax.nn.silu(gate_part) * up_part).astype(jnp.bfloat16)
    terms = jnp.dot(
        hidden,
        lax.all_gather(down_weight, "dp", axis=1, tiled=True),
        preferred_element_type=jnp.float32,
    )
    result = summed_rows(terms, TENSOR, (1, 0), 1).astype(jnp.bfloat16)
    return result


def solution(mesh):
    split = Mesh(
        mesh.devices.reshape(mesh.shape["groups"], mesh.shape["dp"], 32, 2),
        ("groups", "dp", "tensor_0", "tensor_1"),
    )
    placed = (P(("groups", "dp"), TENSOR), P("dp", TENSOR), P(TENSOR, "dp"))
    return jax.shard_map(
        per_device,
        mesh=split,
        in_specs=placed,
        out_specs=P(("groups", "dp"), TENSOR),
        check_vma=False,
    )
```

profile of v0, /device:TPU:34, one launch (start us, length us, event | category | flops | bytes accessed | tf_op | source)
XLA Modules:
  0.0 427.3 jit_solution(7535571929986580808)
XLA Ops:
  6.5 0.0 copy-start
  6.6 0.0 all-gather.3.cloned.1.call-start
  6.6 1.6 copy.5
  8.2 0.1 all-gather.3.cloned.1.call-update
  8.2 0.1 all-gather.5.cloned.1.call-start
  8.3 0.7 all-gather.5.cloned.1.call-update
  9.1 0.1 reduce-scatter.3.cloned.1.call-start
  9.1 160.0 %all-gather.3.cloned.1.call-done = bf16[128,8192]{0,1:T(8,128)(2,1)} async-done(((bf16[128,128]{0,1:T(8,128)(2,1)}), bf16[128,8192]{0,1:T(8,128)(2,1)}) %all-gather.3.cloned.1.call-update) | async-done | bytes 2097168 | tf_op jit(solution)/shard_map/all_gather | solution.py:38
  169.1 4.0 copy.6
  173.1 41.2 %all_to_all.21 = bf16[128,4,2048]{2,0,1:T(8,128)(2,1)S(1)} all-to-all(bf16[128,4,2048]{2,0,1:T(8,128)(2,1)} %copy.6), channel_id=1, replica_groups=mesh['groups'=2,'dp'=4,'tensor_0'=32,'tensor_1'=2] {'dp'}, dimensions={1} | all-to-all | bytes 4194304 | tf_op jit(solution)/shard_map/all_to_all | solution.py:39
  214.3 0.0 copy-done
  214.3 1.2 fusion
  215.5 29.6 %all_to_all.22 = f32[4,128,512]{2,1,0:T(8,128)S(1)} all-to-all(f32[4,128,512]{2,1,0:T(8,128)S(1)} %fusion), channel_id=1, replica_groups=mesh['groups'=2,'dp'=4,'tensor_0'=32,'tensor_1'=2] {'dp'}, dimensions={0} | all-to-all | bytes 2097152 | tf_op jit(solution)/shard_map/all_to_all | solution.py:18
  245.1 0.1 reduce_sum.9
  245.2 4.5 %slice.7 = f32[128,256]{1,0:T(8,128)S(1)} slice(f32[128,512]{1,0:T(8,128)S(1)} %reduce_sum.9), slice={[0:128:1], [1:512:2]} | slice | bytes 262144 | tf_op jit(solution)/shard_map/slice | solution.py:43
  249.7 4.5 %slice.6 = f32[128,256]{1,0:T(8,128)S(1)} slice(f32[128,512]{1,0:T(8,128)S(1)} %reduce_sum.9), slice={[0:128:1], [0:512:2]} | slice | bytes 262144 | tf_op jit(solution)/shard_map/slice | solution.py:42
  254.2 0.0 all-gather.5.cloned.1.call-done
  254.2 2.9 convolution_bitcast_fusion
  257.2 0.7 copy.8
  257.9 4.4 %copy.7 = f32[32,2,128,128]{3,2,0,1:T(8,128)} copy(f32[32,2,128,128]{3,1,0,2:T(2,128)S(1)} %bitcast.21) | data formatting | bytes 8388608 | tf_op jit(solution)/shard_map/reshape | solution.py:24
  262.3 0.1 reduce-scatter.3.cloned.1.call-update
  262.3 0.1 reduce-scatter.5.cloned.1.call-start
  262.4 15.9 %reduce-scatter.3.cloned.1.call-done = f32[32,128,128]{2,1,0:T(8,128)} async-done(((f32[64,128,128]{2,1,0:T(8,128)}), f32[32,128,128]{2,1,0:T(8,128)}) %reduce-scatter.3.cloned.1.call-update) | async-done | bytes 2097168 | tf_op jit(solution)/shard_map/reduce_scatter | solution.py:28
  278.3 0.1 reduce-scatter.5.cloned.1.call-update
  278.4 141.0 %reduce-scatter.5.cloned.1.call-done = f32[1,128,128]{2,1,0:T(8,128)} async-done(((f32[32,128,128]{2,1,0:T(8,128)}), f32[1,128,128]{2,1,0:T(8,128)}) %reduce-scatter.5.cloned.1.call-update) | async-done | bytes 65552 | tf_op jit(solution)/shard_map/reduce_scatter | solution.py:28
  419.3 1.5 convert_bitcast_fusion
Async XLA Ops:
  6.5 207.8 %copy-start = (bf16[2048,512]{1,0:T(8,128)(2,1)S(1)}, bf16[2048,512]{1,0:T(8,128)(2,1)}, u32[]{:S(2)}) copy-start(bf16[2048,512]{1,0:T(8,128)(2,1)} %param.4) | copy-start | bytes 6291460
  6.6 162.5 %all-gather.3.cloned.1.call-start = ((), (), s32[]{:S(2)}) async-start(), calls=%async_computation.4 | async-start | bytes 2129920 | tf_op jit(solution)/shard_map/all_gather | solution.py:38
  8.2 246.0 %all-gather.5.cloned.1.call-start = ((), (), s32[]{:S(2)}) async-start(), calls=%async_computation.5 | async-start | bytes 5242880 | tf_op jit(solution)/shard_map/all_gather | solution.py:47
  9.1 269.2 %reduce-scatter.3.cloned.1.call-start = ((), (), s32[]{:S(2)}) async-start(), calls=%async_computation.6 | async-start | bytes 6291456 | tf_op jit(solution)/shard_map/reduce_scatter | solution.py:28
  262.3 157.0 %reduce-scatter.5.cloned.1.call-start = ((), (), s32[]{:S(2)}) async-start(), calls=%async_computation.7 | async-start | bytes 2162688 | tf_op jit(solution)/shard_map/reduce_scatter | solution.py:28
Sparse Core Ops, SparseCore 0:
  9.5 159.5 all-gather.2
  171.2 76.5 all-gather.4
  262.5 15.7 reduce-scatter.2
  281.0 138.3 reduce-scatter.4
where the time goes:
time: 428 us; the launch traced here: 427 us
  waiting for transfers between devices  318 us (74%)
  blocking collectives  70.8 us (17%)
  local copies, waits for them, and re-layouts  19.7 us (5%)
  between operations  13.2 us (3%)
    all_gather x1, waiting for transfers between devices, per_device(): whole = lax.all_gather(tokens, TENSOR, axis=1, tiled=True)  160 us
    reduce_scatter x2, waiting for transfers between devices, reduced_to_own(): pieces = lax.psum_scatter(pieces, axes[k], scatter_dimension=0, tiled=True)  157 us
    all_to_all x1, blocking collectives, per_device(): lax.all_to_all(whole, 'dp', split_axis=1, concat_axis=0, tiled=True)  41.2 us
    all_to_all x1, blocking collectives, summed_on_arrival(): lax.all_to_all(pieces, axis, split_axis=0, concat_axis=0, tiled=True)  29.6 us
  transfers between devices with their start and end apart: 4, of which 3 were waited for; matrix products, arithmetic and copies ran while one was open for 3% of the time, Pallas kernels for 0%

commit v1 on v0

--- a/solution.py
+++ b/solution.py
@@ -35,7 +35,9 @@
 
 
 def per_device(tokens, gate_up_weight, down_weight):
-    whole = lax.all_gather(tokens, TENSOR, axis=1, tiled=True)
+    whole = jnp.concatenate(
+        lax.all_to_all(jnp.stack([tokens] * lax.axis_size(TENSOR)), TENSOR, 0, 0), axis=1
+    )
     blocks = lax.all_to_all(whole, "dp", split_axis=1, concat_axis=0, tiled=True)
     partial_value = jnp.dot(blocks, gate_up_weight, preferred_element_type=jnp.float32)
     combined = summed_on_arrival(partial_value, "dp", 0)

time: 428 us -> 487 us (1.14)
  starting transfers between devices: 0.19 us -> 47.6 us
  waiting for transfers between devices: 318 us -> 357 us
  blocking collectives: 70.8 us -> 41.9 us
    all_to_all x0 -> x1, waiting for transfers between devices: none -> 198 us  [per_device(): lax.all_to_all(jnp.stack([tokens] * lax.axis_size(TENSOR)), TENSOR, 0, 0)]
    all_gather x1 -> x0, waiting for transfers between devices: 160 us -> none  [per_device(): whole = lax.all_gather(tokens, TENSOR, axis=1, tiled=True)]
    all_to_all x0 -> x1, starting transfers between devices: none -> 47.4 us  [per_device(): lax.all_to_all(jnp.stack([tokens] * lax.axis_size(TENSOR)), TENSOR, 0, 0)]
    all_to_all x1, blocking collectives: 29.6 us -> 14.4 us  [summed_on_arrival(): lax.all_to_all(pieces, axis, split_axis=0, concat_axis=0, tiled=True)]
    all_to_all x1, blocking collectives: 41.2 us -> 27.5 us  [per_device(): lax.all_to_all(whole, 'dp', split_axis=1, concat_axis=0, tiled=True)]
where the time goes in v1:
time: 487 us
  waiting for transfers between devices  357 us (73%)
  starting transfers between devices  47.6 us (10%)
  blocking collectives  41.9 us (9%)
  local copies, waits for them, and re-layouts  21 us (4%)
  between operations  13.2 us (3%)
    all_to_all x1, waiting for transfers between devices, per_device(): lax.all_to_all(jnp.stack([tokens] * lax.axis_size(TENSOR)), TENSOR, 0, 0)  198 us
    reduce_scatter x2, waiting for transfers between devices, reduced_to_own(): pieces = lax.psum_scatter(pieces, axes[k], scatter_dimension=0, tiled=True)  158 us
    all_to_all x1, starting transfers between devices, per_device(): lax.all_to_all(jnp.stack([tokens] * lax.axis_size(TENSOR)), TENSOR, 0, 0)  47.4 us
    all_to_all x1, blocking collectives, per_device(): lax.all_to_all(whole, 'dp', split_axis=1, concat_axis=0, tiled=True)  27.5 us
    all_to_all x1, blocking collectives, summed_on_arrival(): lax.all_to_all(pieces, axis, split_axis=0, concat_axis=0, tiled=True)  14.4 us
  transfers between devices with their start and end apart: 4, of which 3 were waited for; matrix products, arithmetic and copies ran while one was open for 3% of the time, Pallas kernels for 0%

profile of v1, /device:TPU:34, one launch (start us, length us, event | category | flops | bytes accessed | tf_op | source)
XLA Modules:
  0.0 486.5 jit_solution(14032892724918325018)
XLA Ops:
  6.5 0.0 copy-start
  6.6 1.0 copy.5
  7.6 1.9 stack.2
  9.4 47.4 %all-to-all-start = ((bf16[64,128,128]{1,2,0:T(8,128)(2,1)}), bf16[64,128,128]{1,2,0:T(8,128)(2,1)}, u32[]{:S(2)}, u32[]{:S(2)}) async-start(bf16[64,128,128]{1,2,0:T(8,128)(2,1)} %stack.2), calls=%async_computation | async-start | bytes 4194304 | tf_op jit(solution)/shard_map/all_to_all | solution.py:39
  56.8 0.1 all-gather.2.cloned.1.call-start
  56.9 0.7 all-gather.2.cloned.1.call-update
  57.6 0.1 reduce-scatter.3.cloned.1.call-start
  57.7 198.2 %all-to-all-done = bf16[64,128,128]{1,2,0:T(8,128)(2,1)} async-done(((bf16[64,128,128]{1,2,0:T(8,128)(2,1)}), bf16[64,128,128]{1,2,0:T(8,128)(2,1)}, u32[]{:S(2)}, u32[]{:S(2)}) %all-to-all-start) | async-done | bytes 2097184 | tf_op jit(solution)/shard_map/all_to_all | solution.py:39
  255.9 4.0 copy.6
  259.9 27.5 %all_to_all.26 = bf16[128,4,2048]{2,0,1:T(8,128)(2,1)S(1)} all-to-all(bf16[128,4,2048]{2,0,1:T(8,128)(2,1)} %copy.6), channel_id=1, replica_groups=mesh['groups'=2,'dp'=4,'tensor_0'=32,'tensor_1'=2] {'dp'}, dimensions={1} | all-to-all | bytes 4194304 | tf_op jit(solution)/shard_map/all_to_all | solution.py:41
  287.5 0.0 copy-done
  287.5 1.2 fusion
  288.7 14.4 %all_to_all.27 = f32[4,128,512]{2,1,0:T(8,128)S(1)} all-to-all(f32[4,128,512]{2,1,0:T(8,128)S(1)} %fusion), channel_id=1, replica_groups=mesh['groups'=2,'dp'=4,'tensor_0'=32,'tensor_1'=2] {'dp'}, dimensions={0} | all-to-all | bytes 2097152 | tf_op jit(solution)/shard_map/all_to_all | solution.py:18
  303.1 0.1 reduce_sum.9
  303.2 4.5 slice.7
  307.7 4.5 slice.6
  312.2 0.0 all-gather.2.cloned.1.call-done
  312.2 2.9 convolution_bitcast_fusion
  315.1 0.7 copy.8
  315.9 4.4 copy.7
  320.3 0.1 reduce-scatter.3.cloned.1.call-update
  320.3 0.1 reduce-scatter.5.cloned.1.call-start
  320.4 17.1 %reduce-scatter.3.cloned.1.call-done = f32[32,128,128]{2,1,0:T(8,128)} async-done(((f32[64,128,128]{2,1,0:T(8,128)}), f32[32,128,128]{2,1,0:T(8,128)}) %reduce-scatter.3.cloned.1.call-update) | async-done | bytes 2097168 | tf_op jit(solution)/shard_map/reduce_scatter | solution.py:28
  337.5 0.1 reduce-scatter.5.cloned.1.call-update
  337.6 140.9 %reduce-scatter.5.cloned.1.call-done = f32[1,128,128]{2,1,0:T(8,128)} async-done(((f32[32,128,128]{2,1,0:T(8,128)}), f32[1,128,128]{2,1,0:T(8,128)}) %reduce-scatter.5.cloned.1.call-update) | async-done | bytes 65552 | tf_op jit(solution)/shard_map/reduce_scatter | solution.py:28
  478.5 1.5 convert_bitcast_fusion
Async XLA Ops:
  6.5 280.9 %copy-start = (bf16[2048,512]{1,0:T(8,128)(2,1)S(1)}, bf16[2048,512]{1,0:T(8,128)(2,1)}, u32[]{:S(2)}) copy-start(bf16[2048,512]{1,0:T(8,128)(2,1)} %param.4) | copy-start | bytes 6291460
  9.4 246.5 %all-to-all-start = ((bf16[64,128,128]{1,2,0:T(8,128)(2,1)}), bf16[64,128,128]{1,2,0:T(8,128)(2,1)}, u32[]{:S(2)}, u32[]{:S(2)}) async-start(bf16[64,128,128]{1,2,0:T(8,128)(2,1)} %stack.2), calls=%async_computation | async-start | bytes 4194304 | tf_op jit(solution)/shard_map/all_to_all | solution.py:39
  56.8 255.4 %all-gather.2.cloned.1.call-start = ((), (), s32[]{:S(2)}) async-start(), calls=%async_computation.5 | async-start | bytes 5242880 | tf_op jit(solution)/shard_map/all_gather | solution.py:49
  57.6 279.9 %reduce-scatter.3.cloned.1.call-start = ((), (), s32[]{:S(2)}) async-start(), calls=%async_computation.6 | async-start | bytes 6291456 | tf_op jit(solution)/shard_map/reduce_scatter | solution.py:28
  320.3 158.2 %reduce-scatter.5.cloned.1.call-start = ((), (), s32[]{:S(2)}) async-start(), calls=%async_computation.7 | async-start | bytes 2162688 | tf_op jit(solution)/shard_map/reduce_scatter | solution.py:28
Sparse Core Ops, SparseCore 0:
  59.7 64.2 all-gather.1
  320.4 17.0 reduce-scatter.2
  340.4 138.1 reduce-scatter.4
